TPU v7x, 32 devices: a whole 2x2x4 slice. The times are simulated.
32 devices in a mesh: zero: 2 (over core), tp: 4 (over y, x), site: 4 (over z).
Axes of the slice: x: 2, y: 2, z: 4, core: 2. Of those that a mesh axis runs over, the one named last changes fastest.
Arguments:
- weight_gate: float32 [8192, 8192], P(('site', 'zero'), 'tp'), parts along dimension 0, may hold values from -0.1875 to 0.1875
- moment_gate: float32 [8192, 8192], P(('site', 'zero'), 'tp'), parts along dimension 0, may hold values from -0.125 to 0.125
- square_gate: float32 [8192, 8192], P(('site', 'zero'), 'tp'), parts along dimension 0, may hold values from -0.125 to 0.125
- weight_up: float32 [8192, 8192], P(('site', 'zero'), 'tp'), parts along dimension 0, may hold values from -0.1875 to 0.1875
- moment_up: float32 [8192, 8192], P(('site', 'zero'), 'tp'), parts along dimension 0, may hold values from -0.125 to 0.125
- square_up: float32 [8192, 8192], P(('site', 'zero'), 'tp'), parts along dimension 0, may hold values from -0.125 to 0.125
- norm_train: float32 [8192], P(('site', 'zero', 'tp')), parts along dimension 0, may hold values from 0.25 to 1.75
- norm_step: float32 [8192], P(('site', 'zero', 'tp')), parts along dimension 0, may hold values from -0.3 to 0.3
Outputs:
- ready_gate: bfloat16 [8192, 8192], P('site', 'tp'), parts along dimension 0
- ready_up: bfloat16 [8192, 8192], P('site', 'tp'), parts along dimension 0
- scale_gate: float32 [32768], P(('site', 'tp')), parts along dimension 0
- scale_up: float32 [32768], P(('site', 'tp')), parts along dimension 0
- serve_norm: bfloat16 [8192], P('site'), parts along dimension 0
- latest_gate: float32 [8192, 8192], P(('site', 'zero'), 'tp'), parts along dimension 0
- latest_up: float32 [8192, 8192], P(('site', 'zero'), 'tp'), parts along dimension 0
There are 4 independent parts, one for each index of `site`. A program takes and returns all parts, laid end to end along the dimension named above; each array names one. Nothing has to cross between parts.
All inputs are finite; a program needn't handle non-finite values. Where the computation divides by a largest or mean magnitude, that divisor is 1e-20 or more.
Results may differ from a plain program's by a relative error of at most 0.001.
Values may be sent and summed in bfloat16 or wider, within the bound.
A program may use at most 192 MiB of HBM per device.

v0:
```python
import functools

import jax
import jax.numpy as jnp
from jax import lax
from jax.experimental import pallas as pl
from jax.experimental.pallas import tpu as pltpu
from jax.sharding import PartitionSpec as P

learn_rate = 0.25
hold_rate = 0.9
MESH = pl.DeviceIdType.MESH
SLOTS = 4
CHUNK = 1 << 18
BODY = 1 << 16
SPLIT = 4
NORM_AT = 2
READS = 1
SENDS = 4


def step_kernel(
    n, ntp, wide, height,
    wg, mg, sg, wu, mu, su, nt, ns,
    latest_g, latest_u, ready_g, ready_u, scale_g, scale_u, norm,
    held, peaks, norms, parts, in_sem, part_sem, peak_send, peak_recv, ready_send, ready_recv, norm_send, norm_recv,
):
    rows, columns = wg.shape
    chunks = columns // wide
    steps = 2 * chunks
    tall = rows // READS
    long = rows // SENDS
    group = n * ntp
    zero, tp = lax.axis_index("zero"), lax.axis_index("tp")
    me = zero * ntp + tp
    operands = ((wg, mg, sg), (wu, mu, su))
    latest, ready, scale = (latest_g, latest_u), (ready_g, ready_u), (scale_g, scale_u)

    def reads(s, which, p):
        slot = lax.rem(s, SLOTS)
        at = pl.ds(pl.multiple_of((s // 2) * wide, wide), wide)
        here = pl.ds(pl.multiple_of(p * tall, tall), tall)
        return [
            pltpu.make_async_copy(ref.at[here, at], held.at[slot, k, here], in_sem.at[slot, p, k])
            for k, ref in enumerate(operands[which])
        ]

    def member(d):
        return {"zero": lax.rem(zero + d, n)}

    def other(d):
        to = lax.rem(me + d, group)
        return {"zero": to // ntp, "tp": lax.rem(to, ntp)}

    pieces = [pltpu.make_async_copy(ref, parts.at[k], part_sem.at[k]) for k, ref in enumerate((nt, ns))]
    for copy in pieces:
        copy.start()
    for s in range(min(SLOTS, steps)):
        for p in range(READS):
            for copy in reads(s, s % 2, p):
                copy.start()

    barrier = pltpu.get_barrier_semaphore()

    @pl.loop(1, group)
    def _(d):
        pl.semaphore_signal(barrier, inc=1, device_id=other(d), device_id_type=MESH)


    def norm_copy(d):
        return pltpu.make_async_remote_copy(
            src_ref=norms.at[me], dst_ref=norms.at[me],
            send_sem=norm_send.at[d - 1], recv_sem=norm_recv.at[d - 1],
            device_id=other(d), device_id_type=MESH,
        )

    def send_norm():
        for copy in pieces:
            copy.wait()
        norms[me] = parts[0] + parts[1]

        @pl.loop(1, group)
        def _(d):
            norm_copy(d).start()

    def peak_copy(s, d):
        return pltpu.make_async_remote_copy(
            src_ref=peaks.at[s, zero], dst_ref=peaks.at[s, zero],
            send_sem=peak_send.at[s, d - 1], recv_sem=peak_recv.at[s, d - 1],
            device_id=member(d), device_id_type=MESH,
        )

    def ready_copy(s, which, d, p=None):
        begin, many = (zero * rows, rows) if p is None else (zero * rows + p * long, long)
        block = ready[which].at[
            pl.ds(pl.multiple_of(begin, many), many), pl.ds(pl.multiple_of((s // 2) * wide, wide), wide)
        ]
        return pltpu.make_async_remote_copy(
            src_ref=block, dst_ref=block,
            send_sem=ready_send.at[s, d - 1], recv_sem=ready_recv.at[s, d - 1],
            device_id=member(d), device_id_type=MESH,
        )

    def update(s, which):
        slot = lax.rem(s, SLOTS)
        at = pl.ds(pl.multiple_of((s // 2) * wide, wide), wide)
        def part(i, peak):
            here = pl.ds(pl.multiple_of(i * height, height), height)
            hold = hold_rate * held[slot, 1, here, :] + held[slot, 2, here, :]
            new = held[slot, 0, here, :] - learn_rate * hold
            latest[which][here, at] = new
            return jnp.maximum(peak, jnp.max(jnp.abs(new).reshape(height // 8, 8, wide), axis=0))

        def piece(p, peak):
            for copy in reads(s, which, p):
                copy.wait()
            peak = lax.fori_loop(p * (tall // height), (p + 1) * (tall // height), part, peak)

            @pl.when(s + SLOTS < steps)
            def _():
                for copy in reads(s + SLOTS, which, p):
                    copy.start()

            return peak

        peaks[s, zero] = lax.fori_loop(0, READS, piece, jnp.zeros((8, wide), jnp.float32))


    def finish(s, which):
        at = pl.ds(pl.multiple_of((s // 2) * wide, wide), wide)
        for d in range(1, n):
            peak_copy(s, d).wait_recv()
        peak = peaks[s, 0]
        for k in range(1, n):
            peak = jnp.maximum(peak, peaks[s, k])
        top = jnp.max(peak, axis=0, keepdims=True)
        for k in range(wide // 128):
            scale[which][pl.ds((s // 2) * (wide // 128) + k, 1), :] = top[:, k * 128 : (k + 1) * 128]
        inverse = jnp.broadcast_to(1.0 / top, (8, wide))

        def part(i, carry):
            here = pl.ds(pl.multiple_of(i * height, height), height)
            there = pl.ds(pl.multiple_of(zero * rows + i * height, height), height)
            value = latest[which][here, at].reshape(height // 8, 8, wide) * inverse
            ready[which][there, at] = value.reshape(height, wide).astype(jnp.bfloat16)
            return carry

        def piece(p, carry):
            lax.fori_loop(p * (long // height), (p + 1) * (long // height), part, 0)
            for d in range(1, n):
                ready_copy(s, which, d, p).start()
            return carry

        lax.fori_loop(0, SENDS, piece, 0)

    def tell(s):
        for d in range(1, n):
            peak_copy(s, d).start()

    update(0, 0)

    @pl.loop(0, chunks)
    def _(j):
        update(2 * j + 1, 1)

        @pl.when(j == 0)
        def _():
            pl.semaphore_wait(barrier, group - 1)
            tell(0)

        tell(2 * j + 1)
        finish(2 * j, 0)

        @pl.when(j == min(NORM_AT, chunks - 1))
        def _():
            send_norm()

        @pl.when(j < chunks - 1)
        def _():
            update(2 * j + 2, 0)
            tell(2 * j + 2)

        finish(2 * j + 1, 1)

    @pl.loop(1, group)
    def _(d):
        norm_copy(d).wait()

    lines = nt.shape[0]
    for k in range(group):
        norm[k * lines : (k + 1) * lines, :] = norms[k].astype(jnp.bfloat16)
    @pl.loop(0, chunks)
    def _(j):
        for which in range(2):
            for d in range(1, n):
                peak_copy(2 * j + which, d).wait_send()
                ready_copy(2 * j + which, which, d).wait()


def write_kernel(*refs):
    count = len(refs) // 2
    copies = []
    for k in range(count):
        cuts = SPLIT if refs[k].shape[0] % (16 * SPLIT) == 0 else 1
        each = refs[k].shape[0] // cuts
        for cut in range(cuts):
            at = pl.ds(cut * each, each)
            copies.append(pltpu.make_async_copy(refs[k].at[at], refs[count + k].at[at], refs[-1].at[k, cut]))
    for copy in copies:
        copy.start()
    for copy in copies:
        copy.wait()


def per_device(n, ntp, wg, mg, sg, wu, mu, su, norm_train, norm_step):
    rows, columns = wg.shape
    length = norm_train.shape[0]
    lines = pl.cdiv(length, 128)
    as_lines = lambda x: jnp.pad(x, (0, lines * 128 - length)).reshape(lines, 128)
    wide = min(columns, max(128, CHUNK // rows))
    height = min(rows // max(READS, SENDS), max(16, BODY // wide))
    steps = 2 * (columns // wide)
    group = n * ntp
    f32, bf16 = jnp.float32, jnp.bfloat16
    shapes = [
        ((rows, columns), f32),
        ((rows, columns), f32),
        ((n * rows, columns), bf16),
        ((n * rows, columns), bf16),
        ((columns // 128, 128), f32),
        ((columns // 128, 128), f32),
        ((group * lines, 128), bf16),
    ]
    anywhere = pl.BlockSpec(memory_space=pl.ANY)
    vmem = pl.BlockSpec(memory_space=pltpu.VMEM)
    results = pl.pallas_call(
        functools.partial(step_kernel, n, ntp, wide, height),
        out_shape=[pltpu.VMEM(shape, dtype) for shape, dtype in shapes],
        in_specs=[anywhere] * 6 + [pl.BlockSpec(memory_space=pltpu.HBM)] * 2,
        out_specs=[vmem] * len(shapes),
        scratch_shapes=[
            pltpu.VMEM((SLOTS, 3, rows, wide), f32),
            pltpu.VMEM((steps, n, 8, wide), f32),
            pltpu.VMEM((group, lines, 128), f32),
            pltpu.VMEM((2, lines, 128), f32),
            pltpu.SemaphoreType.DMA((SLOTS, READS, 3)),
            pltpu.SemaphoreType.DMA((2,)),
            pltpu.SemaphoreType.DMA((steps, n - 1)),
            pltpu.SemaphoreType.DMA((steps, n - 1)),
            pltpu.SemaphoreType.DMA((steps, n - 1)),
            pltpu.SemaphoreType.DMA((steps, n - 1)),
            pltpu.SemaphoreType.DMA((group - 1,)),
            pltpu.SemaphoreType.DMA((group - 1,)),
        ],
        compiler_params=pltpu.CompilerParams(
            collective_id=0, has_side_effects=True, vmem_limit_bytes=15 << 20
        ),
        name="step",
    )(wg, mg, sg, wu, mu, su, *(pltpu.with_memory_space_constraint(as_lines(x), pltpu.HBM) for x in (norm_train, norm_step)))
    latest_g, latest_u, ready_g, ready_u, scale_g, scale_u, norm = pl.pallas_call(
        write_kernel,
        out_shape=[jax.ShapeDtypeStruct(shape, dtype) for shape, dtype in shapes],
        in_specs=[vmem] * len(shapes),
        out_specs=[anywhere] * len(shapes),
        scratch_shapes=[pltpu.SemaphoreType.DMA((len(shapes), SPLIT))],
        compiler_params=pltpu.CompilerParams(vmem_limit_bytes=2 << 20),
        name="write",
    )(*results)
    return (
        ready_g, ready_u, scale_g.reshape(columns), scale_u.reshape(columns),
        norm.reshape(group, lines * 128)[:, :length].reshape(group * length), latest_g, latest_u,
    )


def solution(mesh):
    block = P(("site", "zero"), "tp")
    return jax.shard_map(
        functools.partial(per_device, mesh.shape["zero"], mesh.shape["tp"]),
        mesh=mesh,
        in_specs=(block,) * 6 + (P(("site", "zero", "tp")),) * 2,
        out_specs=(
            P("site", "tp"), P("site", "tp"), P(("site", "tp")), P(("site", "tp")), P("site"), block, block,
        ),
        check_vma=False,
    )
```

profile of v0, /device:TPU:3, one launch (start us, length us, event | category | flops | bytes accessed | tf_op | source)
XLA Modules:
  0.0 31.7 jit_solution(7499211592556704405)
XLA Ops:
  0.6 19.9 %step.1 = (f32[1024,2048]{1,0:T(8,128)S(1)}, f32[1024,2048]{1,0:T(8,128)S(1)}, bf16[2048,2048]{1,0:T(8,128)(2,1)S(1)}, bf16[2048,2048]{1,0:T(8,128)(2,1)S(1)}, f...) custom-call(f32[1024,2048]{1,0:T(8,128)} %wg.1, f32[1024,2048]{1,0:T(8,128)} %mg.1, ...), custom_call_target="tpu_custom_call" | custom-call | tf_op jit(solution)/shard_map/step/pallas_call | solution.py:236
  20.5 11.2 %write.1 = (f32[1024,2048]{1,0:T(8,128)}, f32[1024,2048]{1,0:T(8,128)}, bf16[2048,2048]{1,0:T(8,128)(2,1)}, bf16[2048,2048]{1,0:T(8,128)(2,1)}, f32[16,128]{1,0:...) custom-call(f32[1024,2048]{1,0:T(8,128)S(1)} %get-tuple-element.21.refs_0_, ...), custom_call_target="tpu_custom_call" | custom-call | tf_op jit(solution)/shard_map/write/pallas_call | solution.py:260
where the time goes:
time: 32.1 us; the launch traced here: 31.7 us
  Pallas kernels  31.1 us (97%)
  between operations  0.64 us (2%)
    pallas_call x1, Pallas kernels, per_device(): pl.pallas_call(functools.partial(step_kernel, n, ntp, wide, height), out_...  19.9 us
    pallas_call x1, Pallas kernels, per_device(): pl.pallas_call(write_kernel, out_shape=[jax.ShapeDtypeStruct(shape, dtype...  11.2 us

commit v1 on v0

--- a/solution.py
+++ b/solution.py
@@ -15,18 +15,20 @@
 BODY = 1 << 16
 SPLIT = 4
 NORM_AT = 2
+LATE = 2
 READS = 1
 SENDS = 4
 
 
 def step_kernel(
-    n, ntp, wide, height,
+    n, ntp, wide, height, late,
     wg, mg, sg, wu, mu, su, nt, ns,
-    latest_g, latest_u, ready_g, ready_u, scale_g, scale_u, norm,
+    latest_g, latest_u, ready_g, ready_u, scale_g, scale_u, norm, sent,
     held, peaks, norms, parts, in_sem, part_sem, peak_send, peak_recv, ready_send, ready_recv, norm_send, norm_recv,
 ):
     rows, columns = wg.shape
     chunks = columns // wide
+    main = chunks - late
     steps = 2 * chunks
     tall = rows // READS
     long = rows // SENDS
@@ -101,7 +103,7 @@
             device_id=member(d), device_id_type=MESH,
         )
 
-    def update(s, which):
+    def update(s, which, t=None):
         slot = lax.rem(s, SLOTS)
         at = pl.ds(pl.multiple_of((s // 2) * wide, wide), wide)
         def part(i, peak):
@@ -109,6 +111,8 @@
             hold = hold_rate * held[slot, 1, here, :] + held[slot, 2, here, :]
             new = held[slot, 0, here, :] - learn_rate * hold
             latest[which][here, at] = new
+            if t is not None:
+                sent[t, here, :] = new
             return jnp.maximum(peak, jnp.max(jnp.abs(new).reshape(height // 8, 8, wide), axis=0))
 
         def piece(p, peak):
@@ -123,8 +127,11 @@
 
             return peak
 
-        peaks[s, zero] = lax.fori_loop(0, READS, piece, jnp.zeros((8, wide), jnp.float32))
-
+        peak = lax.fori_loop(0, READS, piece, jnp.zeros((8, wide), jnp.float32))
+        if t is None:
+            peaks[s, zero] = peak
+        else:
+            sent[t, rows : rows + 8, :] = peak
 
     def finish(s, which):
         at = pl.ds(pl.multiple_of((s // 2) * wide, wide), wide)
@@ -159,7 +166,7 @@
 
     update(0, 0)
 
-    @pl.loop(0, chunks)
+    @pl.loop(0, main)
     def _(j):
         update(2 * j + 1, 1)
 
@@ -171,17 +178,22 @@
         tell(2 * j + 1)
         finish(2 * j, 0)
 
-        @pl.when(j == min(NORM_AT, chunks - 1))
+        @pl.when(j == min(NORM_AT, main - 1))
         def _():
             send_norm()
 
-        @pl.when(j < chunks - 1)
+        @pl.when(j < main - 1)
         def _():
             update(2 * j + 2, 0)
             tell(2 * j + 2)
 
         finish(2 * j + 1, 1)
 
+    @pl.loop(0, late)
+    def _(j):
+        for which in range(2):
+            update(2 * (main + j) + which, which, 2 * j + which)
+
     @pl.loop(1, group)
     def _(d):
         norm_copy(d).wait()
@@ -189,7 +201,7 @@
     lines = nt.shape[0]
     for k in range(group):
         norm[k * lines : (k + 1) * lines, :] = norms[k].astype(jnp.bfloat16)
-    @pl.loop(0, chunks)
+    @pl.loop(0, main)
     def _(j):
         for which in range(2):
             for d in range(1, n):
@@ -197,17 +209,67 @@
                 ready_copy(2 * j + which, which, d).wait()
 
 
-def write_kernel(*refs):
-    count = len(refs) // 2
+def spread(copies, source, target, sem, cuts):
+    each = source.shape[0] // cuts
+    for cut in range(cuts):
+        at = pl.ds(cut * each, each)
+        there = (at, pl.ds(0, source.shape[1]))
+        copies.append(pltpu.make_async_copy(source.at[at], target.at[there], sem.at[cut]))
+
+
+def early_kernel(latest_g, latest_u, ready_g, out_latest_g, out_latest_u, out_ready_g, sem):
     copies = []
-    for k in range(count):
-        cuts = SPLIT if refs[k].shape[0] % (16 * SPLIT) == 0 else 1
-        each = refs[k].shape[0] // cuts
-        for cut in range(cuts):
-            at = pl.ds(cut * each, each)
-            copies.append(pltpu.make_async_copy(refs[k].at[at], refs[count + k].at[at], refs[-1].at[k, cut]))
+    for k, (source, target) in enumerate(((latest_g, out_latest_g), (latest_u, out_latest_u), (ready_g, out_ready_g))):
+        spread(copies, source, target, sem.at[k], SPLIT)
     for copy in copies:
         copy.start()
+    for copy in copies:
+        copy.wait()
+
+
+def rest_kernel(n, height, ready_u, scale_g, scale_u, norm, sent, *refs):
+    others, refs = refs[: n - 1], refs[n - 1 :]
+    _, out_ready_g, out_ready_u, out_scale_g, out_scale_u, out_norm, made, tops, sem, more_sem = refs
+    count, tall, wide = sent.shape
+    rows, width = tall - 8, ready_u.shape[1]
+    zero = lax.axis_index("zero")
+    copies = []
+    spread(copies, ready_u, out_ready_u, sem, SPLIT)
+    copies.append(pltpu.make_async_copy(norm, out_norm, more_sem.at[count]))
+    for copy in copies:
+        copy.start()
+    tops[0] = scale_g[...]
+    tops[1] = scale_u[...]
+    members = (sent, *others)
+
+    for t in range(count):
+        peak = sent[t, rows : rows + 8, :]
+        for other in others:
+            peak = jnp.maximum(peak, other[t, rows : rows + 8, :])
+        top = jnp.max(peak, axis=0, keepdims=True)
+        at = width + (t // 2) * wide
+        for k in range(wide // 128):
+            tops[t % 2, pl.ds(at // 128 + k, 1), :] = top[:, k * 128 : (k + 1) * 128]
+        inverse = jnp.broadcast_to(1.0 / top, (8, wide))
+        for d, member in enumerate(members):
+            owner = lax.rem(zero + n - d, n)
+
+            def part(i, carry, t=t, member=member, owner=owner, inverse=inverse):
+                here = pl.ds(pl.multiple_of(i * height, height), height)
+                there = pl.ds(pl.multiple_of(owner * rows + i * height, height), height)
+                value = member[t, here, :].reshape(height // 8, 8, wide) * inverse
+                made[t, there, :] = value.reshape(height, wide).astype(jnp.bfloat16)
+                return carry
+
+            lax.fori_loop(0, rows // height, part, 0)
+        target = (out_ready_g, out_ready_u)[t % 2].at[:, pl.ds(at, wide)]
+        copy = pltpu.make_async_copy(made.at[t], target, more_sem.at[t])
+        copy.start()
+        copies.append(copy)
+    for k, target in enumerate((out_scale_g, out_scale_u)):
+        copy = pltpu.make_async_copy(tops.at[k], target, more_sem.at[count + 1 + k])
+        copy.start()
+        copies.append(copy)
     for copy in copies:
         copy.wait()
 
@@ -217,11 +279,16 @@
     length = norm_train.shape[0]
     lines = pl.cdiv(length, 128)
     as_lines = lambda x: jnp.pad(x, (0, lines * 128 - length)).reshape(lines, 128)
-    wide = min(columns, max(128, CHUNK // rows))
+    wide = max(128, min(columns // 4, CHUNK // rows))
     height = min(rows // max(READS, SENDS), max(16, BODY // wide))
-    steps = 2 * (columns // wide)
+    chunks = columns // wide
+    late = max(1, chunks * LATE // 8)
+    main = chunks - late
+    assert main > 0
+    steps = 2 * main
     group = n * ntp
     f32, bf16 = jnp.float32, jnp.bfloat16
+    dma = pltpu.SemaphoreType.DMA
     shapes = [
         ((rows, columns), f32),
         ((rows, columns), f32),
@@ -231,41 +298,64 @@
         ((columns // 128, 128), f32),
         ((group * lines, 128), bf16),
     ]
+    between = list(shapes)
+    between[2] = between[3] = ((n * rows, main * wide), bf16)
+    between.append(((2 * late, rows + 8, wide), f32))
     anywhere = pl.BlockSpec(memory_space=pl.ANY)
     vmem = pl.BlockSpec(memory_space=pltpu.VMEM)
-    results = pl.pallas_call(
-        functools.partial(step_kernel, n, ntp, wide, height),
-        out_shape=[pltpu.VMEM(shape, dtype) for shape, dtype in shapes],
+    latest_g, latest_u, ready_g, ready_u, scale_g, scale_u, norm, sent = pl.pallas_call(
+        functools.partial(step_kernel, n, ntp, wide, height, late),
+        out_shape=[pltpu.VMEM(shape, dtype) for shape, dtype in between],
         in_specs=[anywhere] * 6 + [pl.BlockSpec(memory_space=pltpu.HBM)] * 2,
-        out_specs=[vmem] * len(shapes),
+        out_specs=[vmem] * len(between),
         scratch_shapes=[
             pltpu.VMEM((SLOTS, 3, rows, wide), f32),
             pltpu.VMEM((steps, n, 8, wide), f32),
             pltpu.VMEM((group, lines, 128), f32),
             pltpu.VMEM((2, lines, 128), f32),
-            pltpu.SemaphoreType.DMA((SLOTS, READS, 3)),
-            pltpu.SemaphoreType.DMA((2,)),
-            pltpu.SemaphoreType.DMA((steps, n - 1)),
-            pltpu.SemaphoreType.DMA((steps, n - 1)),
-            pltpu.SemaphoreType.DMA((steps, n - 1)),
-            pltpu.SemaphoreType.DMA((steps, n - 1)),
-            pltpu.SemaphoreType.DMA((group - 1,)),
-            pltpu.SemaphoreType.DMA((group - 1,)),
+            dma((SLOTS, READS, 3)),
+            dma((2,)),
+            dma((steps, n - 1)),
+            dma((steps, n - 1)),
+            dma((steps, n - 1)),
+            dma((steps, n - 1)),
+            dma((group - 1,)),
+            dma((group - 1,)),
         ],
         compiler_params=pltpu.CompilerParams(
-            collective_id=0, has_side_effects=True, vmem_limit_bytes=15 << 20
+            collective_id=0, has_side_effects=True, vmem_limit_bytes=14 << 20
         ),
         name="step",
     )(wg, mg, sg, wu, mu, su, *(pltpu.with_memory_space_constraint(as_lines(x), pltpu.HBM) for x in (norm_train, norm_step)))
-    latest_g, latest_u, ready_g, ready_u, scale_g, scale_u, norm = pl.pallas_call(
-        write_kernel,
-        out_shape=[jax.ShapeDtypeStruct(shape, dtype) for shape, dtype in shapes],
-        in_specs=[vmem] * len(shapes),
-        out_specs=[anywhere] * len(shapes),
-        scratch_shapes=[pltpu.SemaphoreType.DMA((len(shapes), SPLIT))],
-        compiler_params=pltpu.CompilerParams(vmem_limit_bytes=2 << 20),
-        name="write",
-    )(*results)
+    others = [lax.ppermute(sent, "zero", [(k, (k + d) % n) for k in range(n)]) for d in range(1, n)]
+    costs = lambda size: pl.CostEstimate(flops=0, bytes_accessed=2 * size, transcendentals=0)
+    as_out = lambda *k: [jax.ShapeDtypeStruct(*shapes[i]) for i in k]
+    latest_g, latest_u, ready_g = pl.pallas_call(
+        early_kernel,
+        out_shape=as_out(0, 1, 2),
+        in_specs=[vmem] * 3,
+        out_specs=[anywhere] * 3,
+        scratch_shapes=[dma((3, SPLIT))],
+        compiler_params=pltpu.CompilerParams(vmem_limit_bytes=1 << 20),
+        cost_estimate=costs(12 * rows * columns),
+        name="early",
+    )(latest_g, latest_u, ready_g)
+    ready_g, ready_u, scale_g, scale_u, norm = pl.pallas_call(
+        functools.partial(rest_kernel, n, height),
+        out_shape=as_out(2, 3, 4, 5, 6),
+        in_specs=[vmem] * (5 + n - 1) + [anywhere],
+        out_specs=[anywhere] * 5,
+        input_output_aliases={5 + n - 1: 0},
+        scratch_shapes=[
+            pltpu.VMEM((2 * late, n * rows, wide), bf16),
+            pltpu.VMEM((2, columns // 128, 128), f32),
+            dma((SPLIT,)),
+            dma((2 * late + 3,)),
+        ],
+        compiler_params=pltpu.CompilerParams(vmem_limit_bytes=6 << 20),
+        cost_estimate=costs(4 * rows * columns),
+        name="rest",
+    )(ready_u, scale_g, scale_u, norm, sent, *others, ready_g)
     return (
         ready_g, ready_u, scale_g.reshape(columns), scale_u.reshape(columns),
         norm.reshape(group, lines * 128)[:, :length].reshape(group * length), latest_g, latest_u,

time: 32.1 us -> 30.4 us (0.947)
  Pallas kernels: 31.1 us -> 28.9 us
  starting transfers between devices: 0 us -> 0.74 us
    pallas_call x2 -> x3, Pallas kernels: 31.1 us -> 28.9 us  [the longest x1 17 us: per_device(): pl.pallas_call(functools.partial(step_kernel, n, ntp, wide, height, late)...]
    ppermute x0 -> x1, starting transfers between devices: none -> 0.74 us  [per_device(): lax.ppermute(sent, 'zero', [(k, (k + d) % n) for k in range(n)])]
  transfers between devices with their start and end apart: 0 -> 1, of which waited for: 0 -> 0; matrix products, arithmetic and copies ran while one was open for 0% -> 0% of each run, Pallas kernels for 0% -> 26%
where the time goes in v1:
time: 30.4 us; the launch traced here: 30.3 us
  Pallas kernels  28.9 us (95%)
  starting transfers between devices  0.74 us (2%)
  between operations  0.66 us (2%)
    pallas_call x1, Pallas kernels, per_device(): pl.pallas_call(functools.partial(step_kernel, n, ntp, wide, height, late)...  17 us
    pallas_call x1, Pallas kernels, per_device(): pl.pallas_call(early_kernel, out_shape=as_out(0, 1, 2), in_specs=[vmem] *...  7.83 us
    pallas_call x1, Pallas kernels, per_device(): pl.pallas_call(functools.partial(rest_kernel, n, height), out_shape=as_ou...  4.05 us
    ppermute x1, starting transfers between devices, per_device(): lax.ppermute(sent, 'zero', [(k, (k + d) % n) for k in range(n)])  0.74 us
  transfers between devices with their start and end apart: 1, of which 0 were waited for; matrix products, arithmetic and copies ran while one was open for 0% of the time, Pallas kernels for 26%

profile of v1, /device:TPU:3, one launch (start us, length us, event | category | flops | bytes accessed | tf_op | source)
XLA Modules:
  0.0 30.3 jit_solution(10329949822579721526)
XLA Ops:
  0.6 17.0 %step.1 = (f32[1024,2048]{1,0:T(8,128)S(1)}, f32[1024,2048]{1,0:T(8,128)S(1)}, bf16[2048,1536]{1,0:T(8,128)(2,1)S(1)}, bf16[2048,1536]{1,0:T(8,128)(2,1)S(1)}, f...) custom-call(f32[1024,2048]{1,0:T(8,128)} %wg.1, ...), custom_call_target="tpu_custom_call" | custom-call | tf_op jit(solution)/shard_map/step/pallas_call | solution.py:306
  17.6 0.7 %collective-permute-start = (f32[4,1032,256]{2,1,0:T(8,128)S(1)}, f32[4,1032,256]{2,1,0:T(8,128)S(1)}, u32[]{:S(2)}, u32[]{:S(2)}) collective-permute-start(f32[4,1032,256]{2,1,0:T(8,128)S(1)} %get-tuple-element.27.sent), channel_id=1, source_target_pairs={{0,16},{16,0},{1,17},{17,1},{2,18},{18,2},{3,19},{19,3},{4,20},{20... | collective-permute-start | bytes 12681224 | tf_op jit(solution)/shard_map/ppermute | solution.py:330
  18.4 7.8 %early.1 = (f32[1024,2048]{1,0:T(8,128)}, f32[1024,2048]{1,0:T(8,128)}, bf16[2048,2048]{1,0:T(8,128)(2,1)}) custom-call(f32[1024,2048]{1,0:T(8,128)S(1)} %get-tuple-element.28.latest_g, f32[1024,2048]{1,0:T(8,128)S(1)} %get-tuple-element.29.latest_u, bf16[2048,1536]{1,0:T(8,128)(2,1)S(1)} %get-tuple-element.30.ready_g), custom_call_target="tpu_custom_call" | custom-call | bytes 50331648 | tf_op jit(solution)/shard_map/early/pallas_call | solution.py:333
  26.2 0.0 collective-permute-done.refs_0_
  26.2 4.1 %rest.1 = (bf16[2048,2048]{1,0:T(8,128)(2,1)}, bf16[2048,2048]{1,0:T(8,128)(2,1)}, f32[16,128]{1,0:T(8,128)}, f32[16,128]{1,0:T(8,128)}, bf16[16,128]{1,0:T(8,128)(2,1)}) custom-call(bf16[2048,1536]{1,0:T(8,128)(2,1)S(1)} %get-tuple-element.23.ready_u, f32[16,128]{1,0:T(8,128)S(1)} %get-tuple-element.24.scale_g, ...), custom_call_target="tpu_custom_call", output_to_operand_aliasing={{0}: (6, {})} | custom-call | bytes 16777216 | tf_op jit(solution)/shard_map/rest/pallas_call | solution.py:343
Async XLA Ops:
  17.6 8.6 %collective-permute-start = (f32[4,1032,256]{2,1,0:T(8,128)S(1)}, f32[4,1032,256]{2,1,0:T(8,128)S(1)}, u32[]{:S(2)}, u32[]{:S(2)}) collective-permute-start(f32[4,1032,256]{2,1,0:T(8,128)S(1)} %get-tuple-element.27.sent), channel_id=1, source_target_pairs={{0,16},{16,0},{1,17},{17,1},{2,18},{18,2},{3,19},{19,3},{4,20},{20... | collective-permute-start | bytes 12681224 | tf_op jit(solution)/shard_map/ppermute | solution.py:330

commit v2 on v1

--- a/solution.py
+++ b/solution.py
@@ -12,12 +12,12 @@
 MESH = pl.DeviceIdType.MESH
 SLOTS = 4
 CHUNK = 1 << 18
-BODY = 1 << 16
+BODY = 1 << 17
 SPLIT = 4
 NORM_AT = 2
 LATE = 2
-READS = 1
-SENDS = 4
+READS = 2
+SENDS = 2
 
 
 def step_kernel(
@@ -43,7 +43,7 @@
         at = pl.ds(pl.multiple_of((s // 2) * wide, wide), wide)
         here = pl.ds(pl.multiple_of(p * tall, tall), tall)
         return [
-            pltpu.make_async_copy(ref.at[here, at], held.at[slot, k, here], in_sem.at[slot, p, k])
+            pltpu.make_async_copy(ref.at[here, at], held.at[slot, k, here], in_sem.at[slot, p])
             for k, ref in enumerate(operands[which])
         ]
 
@@ -69,10 +69,9 @@
         pl.semaphore_signal(barrier, inc=1, device_id=other(d), device_id_type=MESH)
 
 
-    def norm_copy(d):
+    def norm_copy(d, at):
         return pltpu.make_async_remote_copy(
-            src_ref=norms.at[me], dst_ref=norms.at[me],
-            send_sem=norm_send.at[d - 1], recv_sem=norm_recv.at[d - 1],
+            src_ref=norms.at[at], dst_ref=norms.at[at], send_sem=norm_send, recv_sem=norm_recv,
             device_id=other(d), device_id_type=MESH,
         )
 
@@ -83,12 +82,12 @@
 
         @pl.loop(1, group)
         def _(d):
-            norm_copy(d).start()
+            norm_copy(d, me).start()
 
     def peak_copy(s, d):
         return pltpu.make_async_remote_copy(
             src_ref=peaks.at[s, zero], dst_ref=peaks.at[s, zero],
-            send_sem=peak_send.at[s, d - 1], recv_sem=peak_recv.at[s, d - 1],
+            send_sem=peak_send.at[d - 1], recv_sem=peak_recv.at[s, d - 1],
             device_id=member(d), device_id_type=MESH,
         )
 
@@ -99,7 +98,7 @@
         ]
         return pltpu.make_async_remote_copy(
             src_ref=block, dst_ref=block,
-            send_sem=ready_send.at[s, d - 1], recv_sem=ready_recv.at[s, d - 1],
+            send_sem=ready_send.at[which, d - 1], recv_sem=ready_recv.at[which, d - 1],
             device_id=member(d), device_id_type=MESH,
         )
 
@@ -116,8 +115,8 @@
             return jnp.maximum(peak, jnp.max(jnp.abs(new).reshape(height // 8, 8, wide), axis=0))
 
         def piece(p, peak):
-            for copy in reads(s, which, p):
-                copy.wait()
+            landed = held.at[slot, :, pl.ds(pl.multiple_of(p * tall, tall), tall)]
+            pltpu.make_async_copy(landed, landed, in_sem.at[slot, p]).wait()
             peak = lax.fori_loop(p * (tall // height), (p + 1) * (tall // height), part, peak)
 
             @pl.when(s + SLOTS < steps)
@@ -189,40 +188,48 @@
 
         finish(2 * j + 1, 1)
 
+    def close():
+        norm_copy(1, pl.ds(0, group - 1)).wait()
+
+        lines = nt.shape[0]
+        for k in range(group):
+            norm[k * lines : (k + 1) * lines, :] = norms[k].astype(jnp.bfloat16)
+
+
     @pl.loop(0, late)
     def _(j):
+        update(2 * (main + j), 0, 2 * j)
+        pl.when(j == late - 1)(close)
+        update(2 * (main + j) + 1, 1, 2 * j + 1)
+
+    for d in range(1, n):
+        told = peaks.at[:, zero]
+        pltpu.make_async_remote_copy(
+            src_ref=told, dst_ref=told, send_sem=peak_send.at[d - 1], recv_sem=peak_recv.at[0, d - 1],
+            device_id=member(d), device_id_type=MESH,
+        ).wait_send()
         for which in range(2):
-            update(2 * (main + j) + which, which, 2 * j + which)
-
-    @pl.loop(1, group)
-    def _(d):
-        norm_copy(d).wait()
-
-    lines = nt.shape[0]
-    for k in range(group):
-        norm[k * lines : (k + 1) * lines, :] = norms[k].astype(jnp.bfloat16)
-    @pl.loop(0, main)
-    def _(j):
-        for which in range(2):
-            for d in range(1, n):
-                peak_copy(2 * j + which, d).wait_send()
-                ready_copy(2 * j + which, which, d).wait()
-
-
-def spread(copies, source, target, sem, cuts):
-    each = source.shape[0] // cuts
-    for cut in range(cuts):
+            block = ready[which].at[pl.ds(pl.multiple_of(zero * rows, rows), rows)]
+            pltpu.make_async_remote_copy(
+                src_ref=block, dst_ref=block,
+                send_sem=ready_send.at[which, d - 1], recv_sem=ready_recv.at[which, d - 1],
+                device_id=member(d), device_id_type=MESH,
+            ).wait()
+
+
+def spread(source, target, sem):
+    width = pl.ds(0, source.shape[1])
+    each = source.shape[0] // SPLIT
+    for cut in range(SPLIT):
         at = pl.ds(cut * each, each)
-        there = (at, pl.ds(0, source.shape[1]))
-        copies.append(pltpu.make_async_copy(source.at[at], target.at[there], sem.at[cut]))
+        pltpu.make_async_copy(source.at[at], target.at[at, width], sem).start()
+    return pltpu.make_async_copy(source, target.at[:, width], sem)
 
 
 def early_kernel(latest_g, latest_u, ready_g, out_latest_g, out_latest_u, out_ready_g, sem):
     copies = []
     for k, (source, target) in enumerate(((latest_g, out_latest_g), (latest_u, out_latest_u), (ready_g, out_ready_g))):
-        spread(copies, source, target, sem.at[k], SPLIT)
-    for copy in copies:
-        copy.start()
+        copies.append(spread(source, target, sem.at[k]))
     for copy in copies:
         copy.wait()
 
@@ -233,11 +240,8 @@
     count, tall, wide = sent.shape
     rows, width = tall - 8, ready_u.shape[1]
     zero = lax.axis_index("zero")
-    copies = []
-    spread(copies, ready_u, out_ready_u, sem, SPLIT)
-    copies.append(pltpu.make_async_copy(norm, out_norm, more_sem.at[count]))
-    for copy in copies:
-        copy.start()
+    copies = [spread(ready_u, out_ready_u, sem), pltpu.make_async_copy(norm, out_norm, more_sem.at[count])]
+    copies[1].start()
     tops[0] = scale_g[...]
     tops[1] = scale_u[...]
     members = (sent, *others)
@@ -313,14 +317,14 @@
             pltpu.VMEM((steps, n, 8, wide), f32),
             pltpu.VMEM((group, lines, 128), f32),
             pltpu.VMEM((2, lines, 128), f32),
-            dma((SLOTS, READS, 3)),
+            dma((SLOTS, READS)),
             dma((2,)),
+            dma((n - 1,)),
             dma((steps, n - 1)),
-            dma((steps, n - 1)),
-            dma((steps, n - 1)),
-            dma((steps, n - 1)),
-            dma((group - 1,)),
-            dma((group - 1,)),
+            dma((2, n - 1)),
+            dma((2, n - 1)),
+            dma,
+            dma,
         ],
         compiler_params=pltpu.CompilerParams(
             collective_id=0, has_side_effects=True, vmem_limit_bytes=14 << 20
@@ -335,7 +339,7 @@
         out_shape=as_out(0, 1, 2),
         in_specs=[vmem] * 3,
         out_specs=[anywhere] * 3,
-        scratch_shapes=[dma((3, SPLIT))],
+        scratch_shapes=[dma((3,))],
         compiler_params=pltpu.CompilerParams(vmem_limit_bytes=1 << 20),
         cost_estimate=costs(12 * rows * columns),
         name="early",
@@ -349,7 +353,7 @@
         scratch_shapes=[
             pltpu.VMEM((2 * late, n * rows, wide), bf16),
             pltpu.VMEM((2, columns // 128, 128), f32),
-            dma((SPLIT,)),
+            dma,
             dma((2 * late + 3,)),
         ],
         compiler_params=pltpu.CompilerParams(vmem_limit_bytes=6 << 20),

time: 30.4 us -> 29.6 us (0.974)
  Pallas kernels: 28.9 us -> 28.1 us
    pallas_call x1, Pallas kernels: 17 us -> 16.3 us  [per_device(): pl.pallas_call(functools.partial(step_kernel, n, ntp, wide, height, late)...]
where the time goes in v2:
time: 29.6 us; the launch traced here: 29.5 us
  Pallas kernels  28.1 us (95%)
  starting transfers between devices  0.74 us (2%)
  between operations  0.66 us (2%)
    pallas_call x1, Pallas kernels, per_device(): pl.pallas_call(functools.partial(step_kernel, n, ntp, wide, height, late)...  16.3 us
    pallas_call x1, Pallas kernels, per_device(): pl.pallas_call(early_kernel, out_shape=as_out(0, 1, 2), in_specs=[vmem] *...  7.75 us
    pallas_call x1, Pallas kernels, per_device(): pl.pallas_call(functools.partial(rest_kernel, n, height), out_shape=as_ou...  4.03 us
    ppermute x1, starting transfers between devices, per_device(): lax.ppermute(sent, 'zero', [(k, (k + d) % n) for k in range(n)])  0.74 us
  transfers between devices with their start and end apart: 1, of which 0 were waited for; matrix products, arithmetic and copies ran while one was open for 0% of the time, Pallas kernels for 26%

profile of v2, /device:TPU:3, one launch (start us, length us, event | category | flops | bytes accessed | tf_op | source)
XLA Modules:
  0.0 29.5 jit_solution(5101683466062226862)
XLA Ops:
  0.6 16.3 %step.1 = (f32[1024,2048]{1,0:T(8,128)S(1)}, f32[1024,2048]{1,0:T(8,128)S(1)}, bf16[2048,1536]{1,0:T(8,128)(2,1)S(1)}, bf16[2048,1536]{1,0:T(8,128)(2,1)S(1)}, f...) custom-call(f32[1024,2048]{1,0:T(8,128)} %wg.1, ...), custom_call_target="tpu_custom_call" | custom-call | tf_op jit(solution)/shard_map/step/pallas_call | solution.py:310
  16.9 0.7 %collective-permute-start = (f32[4,1032,256]{2,1,0:T(8,128)S(1)}, f32[4,1032,256]{2,1,0:T(8,128)S(1)}, u32[]{:S(2)}, u32[]{:S(2)}) collective-permute-start(f32[4,1032,256]{2,1,0:T(8,128)S(1)} %get-tuple-element.27.sent), channel_id=1, source_target_pairs={{0,16},{16,0},{1,17},{17,1},{2,18},{18,2},{3,19},{19,3},{4,20},{20... | collective-permute-start | bytes 12681224 | tf_op jit(solution)/shard_map/ppermute | solution.py:334
  17.7 7.7 %early.1 = (f32[1024,2048]{1,0:T(8,128)}, f32[1024,2048]{1,0:T(8,128)}, bf16[2048,2048]{1,0:T(8,128)(2,1)}) custom-call(f32[1024,2048]{1,0:T(8,128)S(1)} %get-tuple-element.28.latest_g, f32[1024,2048]{1,0:T(8,128)S(1)} %get-tuple-element.29.latest_u, bf16[2048,1536]{1,0:T(8,128)(2,1)S(1)} %get-tuple-element.30.ready_g), custom_call_target="tpu_custom_call" | custom-call | bytes 50331648 | tf_op jit(solution)/shard_map/early/pallas_call | solution.py:337
  25.4 0.0 collective-permute-done.refs_0_
  25.4 4.0 %rest.1 = (bf16[2048,2048]{1,0:T(8,128)(2,1)}, bf16[2048,2048]{1,0:T(8,128)(2,1)}, f32[16,128]{1,0:T(8,128)}, f32[16,128]{1,0:T(8,128)}, bf16[16,128]{1,0:T(8,128)(2,1)}) custom-call(bf16[2048,1536]{1,0:T(8,128)(2,1)S(1)} %get-tuple-element.23.ready_u, f32[16,128]{1,0:T(8,128)S(1)} %get-tuple-element.24.scale_g, ...), custom_call_target="tpu_custom_call", output_to_operand_aliasing={{0}: (6, {})} | custom-call | bytes 16777216 | tf_op jit(solution)/shard_map/rest/pallas_call | solution.py:347
Async XLA Ops:
  16.9 8.5 %collective-permute-start = (f32[4,1032,256]{2,1,0:T(8,128)S(1)}, f32[4,1032,256]{2,1,0:T(8,128)S(1)}, u32[]{:S(2)}, u32[]{:S(2)}) collective-permute-start(f32[4,1032,256]{2,1,0:T(8,128)S(1)} %get-tuple-element.27.sent), channel_id=1, source_target_pairs={{0,16},{16,0},{1,17},{17,1},{2,18},{18,2},{3,19},{19,3},{4,20},{20... | collective-permute-start | bytes 12681224 | tf_op jit(solution)/shard_map/ppermute | solution.py:334

commit v3 on v2

--- a/solution.py
+++ b/solution.py
@@ -17,6 +17,7 @@
 NORM_AT = 2
 LATE = 2
 READS = 2
+RING = 4
 SENDS = 2
 
 
@@ -54,7 +55,7 @@
         to = lax.rem(me + d, group)
         return {"zero": to // ntp, "tp": lax.rem(to, ntp)}
 
-    pieces = [pltpu.make_async_copy(ref, parts.at[k], part_sem.at[k]) for k, ref in enumerate((nt, ns))]
+    pieces = [pltpu.make_async_copy(ref, parts.at[k], part_sem) for k, ref in enumerate((nt, ns))]
     for copy in pieces:
         copy.start()
     for s in range(min(SLOTS, steps)):
@@ -76,8 +77,7 @@
         )
 
     def send_norm():
-        for copy in pieces:
-            copy.wait()
+        pltpu.make_async_copy(parts, parts, part_sem).wait()
         norms[me] = parts[0] + parts[1]
 
         @pl.loop(1, group)
@@ -87,7 +87,7 @@
     def peak_copy(s, d):
         return pltpu.make_async_remote_copy(
             src_ref=peaks.at[s, zero], dst_ref=peaks.at[s, zero],
-            send_sem=peak_send.at[d - 1], recv_sem=peak_recv.at[s, d - 1],
+            send_sem=peak_send.at[d - 1], recv_sem=peak_recv.at[lax.rem(s, RING), d - 1],
             device_id=member(d), device_id_type=MESH,
         )
 
@@ -318,9 +318,9 @@
             pltpu.VMEM((group, lines, 128), f32),
             pltpu.VMEM((2, lines, 128), f32),
             dma((SLOTS, READS)),
-            dma((2,)),
+            dma,
             dma((n - 1,)),
-            dma((steps, n - 1)),
+            dma((RING, n - 1)),
             dma((2, n - 1)),
             dma((2, n - 1)),
             dma,

time: 29.6 us -> 29.5 us (level)
  no operation moved by 1% of the time
where the time goes in v3:
time: 29.5 us; the launch traced here: 29.4 us
  Pallas kernels  28 us (95%)
  starting transfers between devices  0.74 us (3%)
  between operations  0.66 us (2%)
    pallas_call x1, Pallas kernels, per_device(): pl.pallas_call(functools.partial(step_kernel, n, ntp, wide, height, late)...  16.2 us
    pallas_call x1, Pallas kernels, per_device(): pl.pallas_call(early_kernel, out_shape=as_out(0, 1, 2), in_specs=[vmem] *...  7.75 us
    pallas_call x1, Pallas kernels, per_device(): pl.pallas_call(functools.partial(rest_kernel, n, height), out_shape=as_ou...  4.03 us
    ppermute x1, starting transfers between devices, per_device(): lax.ppermute(sent, 'zero', [(k, (k + d) % n) for k in range(n)])  0.74 us
  transfers between devices with their start and end apart: 1, of which 0 were waited for; matrix products, arithmetic and copies ran while one was open for 0% of the time, Pallas kernels for 26%

profile of v3, /device:TPU:3, one launch (start us, length us, event | category | flops | bytes accessed | tf_op | source)
XLA Modules:
  0.0 29.4 jit_solution(16900718901897712779)
XLA Ops:
  0.6 16.2 %step.1 = (f32[1024,2048]{1,0:T(8,128)S(1)}, f32[1024,2048]{1,0:T(8,128)S(1)}, bf16[2048,1536]{1,0:T(8,128)(2,1)S(1)}, bf16[2048,1536]{1,0:T(8,128)(2,1)S(1)}, f...) custom-call(f32[1024,2048]{1,0:T(8,128)} %wg.1, ...), custom_call_target="tpu_custom_call" | custom-call | tf_op jit(solution)/shard_map/step/pallas_call | solution.py:310
  16.9 0.7 %collective-permute-start = (f32[4,1032,256]{2,1,0:T(8,128)S(1)}, f32[4,1032,256]{2,1,0:T(8,128)S(1)}, u32[]{:S(2)}, u32[]{:S(2)}) collective-permute-start(f32[4,1032,256]{2,1,0:T(8,128)S(1)} %get-tuple-element.27.sent), channel_id=1, source_target_pairs={{0,16},{16,0},{1,17},{17,1},{2,18},{18,2},{3,19},{19,3},{4,20},{20... | collective-permute-start | bytes 12681224 | tf_op jit(solution)/shard_map/ppermute | solution.py:334
  17.6 7.7 %early.1 = (f32[1024,2048]{1,0:T(8,128)}, f32[1024,2048]{1,0:T(8,128)}, bf16[2048,2048]{1,0:T(8,128)(2,1)}) custom-call(f32[1024,2048]{1,0:T(8,128)S(1)} %get-tuple-element.28.latest_g, f32[1024,2048]{1,0:T(8,128)S(1)} %get-tuple-element.29.latest_u, bf16[2048,1536]{1,0:T(8,128)(2,1)S(1)} %get-tuple-element.30.ready_g), custom_call_target="tpu_custom_call" | custom-call | bytes 50331648 | tf_op jit(solution)/shard_map/early/pallas_call | solution.py:337
  25.3 0.0 collective-permute-done.refs_0_
  25.4 4.0 %rest.1 = (bf16[2048,2048]{1,0:T(8,128)(2,1)}, bf16[2048,2048]{1,0:T(8,128)(2,1)}, f32[16,128]{1,0:T(8,128)}, f32[16,128]{1,0:T(8,128)}, bf16[16,128]{1,0:T(8,128)(2,1)}) custom-call(bf16[2048,1536]{1,0:T(8,128)(2,1)S(1)} %get-tuple-element.23.ready_u, f32[16,128]{1,0:T(8,128)S(1)} %get-tuple-element.24.scale_g, ...), custom_call_target="tpu_custom_call", output_to_operand_aliasing={{0}: (6, {})} | custom-call | bytes 16777216 | tf_op jit(solution)/shard_map/rest/pallas_call | solution.py:347
Async XLA Ops:
  16.9 8.5 %collective-permute-start = (f32[4,1032,256]{2,1,0:T(8,128)S(1)}, f32[4,1032,256]{2,1,0:T(8,128)S(1)}, u32[]{:S(2)}, u32[]{:S(2)}) collective-permute-start(f32[4,1032,256]{2,1,0:T(8,128)S(1)} %get-tuple-element.27.sent), channel_id=1, source_target_pairs={{0,16},{16,0},{1,17},{17,1},{2,18},{18,2},{3,19},{19,3},{4,20},{20... | collective-permute-start | bytes 12681224 | tf_op jit(solution)/shard_map/ppermute | solution.py:334
